TPU v7x, 32 devices: a whole 2x2x4 slice. The times are simulated.
32 devices in a mesh: outer: 4 (over y, core), inner: 8 (over z, x).
Axes of the slice: x: 2, y: 2, z: 4, core: 2. Of those that a mesh axis runs over, the one named last changes fastest.
Arguments:
- query_rows: bfloat16 [8192, 1024], P(('outer', 'inner')), may hold values from -6 to 6
- key_rows: bfloat16 [8192, 1024], P(('outer', 'inner')), may hold values from -6 to 6
- value_rows: bfloat16 [8192, 1024], P(('outer', 'inner')), may hold values from -6 to 6
- log_decay: float32 [8, 8192], P(None, ('outer', 'inner')), may hold values from -0.8 to 0, as said below
- grad_out: bfloat16 [8192, 1024], P(('outer', 'inner')), may hold values from -6 to 6
Outputs:
- attended: bfloat16 [8192, 1024], P(('outer', 'inner'))
- grad_queries: bfloat16 [8192, 1024], P(('outer', 'inner'))
- grad_keys: bfloat16 [8192, 1024], P(('outer', 'inner'))
- grad_values: bfloat16 [8192, 1024], P(('outer', 'inner'))
Inputs may be any that keep to these rules, and one draw needn't show every extreme that they name: `log_decay`: every entry is negative.
All inputs are finite; a program needn't handle non-finite values.
Results may differ from a plain program's by a relative error of at most 0.0063.
Values sent between devices are 32-bit elements; how exact they have to be, the bound alone decides.
A program may use at most 320 MiB of HBM per device.

v0:
```python
import functools
import math

import jax
import jax.numpy as jnp
from jax import lax
from jax.experimental import pallas as pl
from jax.experimental.pallas import tpu as pltpu
from jax.sharding import PartitionSpec as P

EPSILON = 1e-06
F32 = jnp.float32
BF16 = jnp.bfloat16
MESH = pl.DeviceIdType.MESH
PARTS = 4


def dot(a, b, da, db):
    return lax.dot_general(a, b, (((da,), (db,)), ((), ())), preferred_element_type=F32)


def kernel(outer_size, inner_size, parts, q_hbm, k_hbm, v_hbm, decay_hbm, g_hbm,
           att_ref, gq_ref, gk_ref, gv_ref,
           q_ref, k_ref, v_ref, decay_ref, g_ref,
           run_ref, col_ref, tot_ref, fac_ref, facs_ref, dec_ref, w_ref, kd_ref, mix_ref, gm_ref,
           send1, recv1, out1, ret1, agg1, send2, recv2, out2, ret2, agg2, ent_ref, gkl_ref, gvl_ref,
           load_sems, fac_sems, send_sems, recv_sems):
    n = outer_size * inner_size
    half_inner = inner_size // 2
    count = n // 2
    heads, tokens = decay_ref.shape
    size = q_ref.shape[1] // heads
    scaling = 1.0 / math.sqrt(size)
    per_head = count // heads
    rows = size // (per_head * parts)
    place_o, place_i = lax.axis_index("outer"), lax.axis_index("inner")
    half = place_i // half_inner
    me = place_o * inner_size + place_i
    seat = place_o * half_inner + place_i % half_inner

    loads = [pltpu.make_async_copy(source, target, load_sems.at[at]) for at, (source, target) in enumerate(
        ((decay_hbm, decay_ref), (k_hbm, k_ref), (v_hbm, v_ref), (q_hbm, q_ref), (g_hbm, g_ref)))]
    for load in loads:
        load.start()

    def everyone(act):
        def turn(i, carry):
            at = (me + 1 + i) % n
            act(at // inner_size, at % inner_size)
            return carry
        lax.fori_loop(0, n - 1, turn, 0)

    def seat_of(o, i):
        return o * half_inner + i % half_inner

    barrier = pltpu.get_barrier_semaphore()
    everyone(lambda o, i: pl.semaphore_signal(barrier, inc=1, device_id=(o, i), device_id_type=MESH))

    def exchange(source, target, phase, part):
        def turn(i, carry):
            step = i + 1
            o = (place_o + step % outer_size) % outer_size
            i = half * half_inner + (place_i % half_inner + step // outer_size) % half_inner
            pltpu.make_async_remote_copy(
                src_ref=source.at[part, seat_of(o, i)], dst_ref=target.at[part, seat],
                send_sem=send_sems.at[phase, part], recv_sem=recv_sems.at[phase, part],
                device_id=(o, i), device_id_type=MESH).start()
            return carry
        lax.fori_loop(0, count - 1, turn, 0)

    def across(sums, phase, part):
        pltpu.make_async_remote_copy(
            src_ref=sums.at[part, half], dst_ref=sums.at[part, half],
            send_sem=send_sems.at[phase, part], recv_sem=recv_sems.at[phase, part],
            device_id=(place_o, (place_i + half_inner) % inner_size), device_id_type=MESH).start()

    def drain(piece, sem):
        pltpu.make_async_copy(piece, piece, sem).wait()

    def others(buffer, part):
        return buffer.at[part, pl.ds(0, count - 1)]

    def each_head(act):
        def turn(i, carry):
            act(2 * i)
            act(2 * i + 1)
            return carry
        lax.fori_loop(0, heads // 2, turn, 0)

    def span(h):
        return pl.ds(pl.multiple_of(h * size, size), size)

    def put_state(target, h, state):
        for p in range(per_head):
            for part in range(parts):
                first = (p * parts + part) * rows
                target[part, h * per_head + p] = state[first:first + rows]

    def get_state(source, h):
        return jnp.concatenate(
            [source[part, h * per_head + p] for p in range(per_head) for part in range(parts)], axis=0)

    loads[0].wait()
    running = decay_ref[...]
    lane = lax.broadcasted_iota(jnp.int32, (heads, tokens), 1)
    shift = 1
    while shift < tokens:
        running = running + jnp.where(lane >= shift, pltpu.roll(running, shift, 1), 0.0)
        shift *= 2
    run_ref[...] = running
    for h in range(heads):
        row = running[h:h + 1]
        col_ref[h] = jnp.broadcast_to(row, (size, tokens)).T
        total = jnp.broadcast_to(row[:, tokens - 1:], (1, size))
        tot_ref[h] = total
        fac_ref[h] = jnp.exp(total)
    loads[1].wait()
    loads[2].wait()

    def state_of(h):
        cols = span(h)
        shrink = jnp.exp(tot_ref[h] - col_ref[h])
        key_dec = (k_ref[:, cols].astype(F32) * shrink).astype(BF16)
        kd_ref[:, cols] = key_dec
        put_state(send1, h, dot(key_dec, v_ref[:, cols], 0, 0))

    each_head(state_of)
    pl.semaphore_wait(barrier, n - 1)

    def send_factor(o, i):
        pltpu.make_async_remote_copy(
            src_ref=fac_ref.at[seat_of(o, i) // per_head], dst_ref=facs_ref.at[me],
            send_sem=fac_sems.at[0], recv_sem=fac_sems.at[1],
            device_id=(o, i), device_id_type=MESH).start()

    exchange(send1, recv1, 0, 0)
    everyone(send_factor)
    for part in range(1, parts):
        exchange(send1, recv1, 0, part)
    facs_ref[me] = fac_ref[seat // per_head]
    for part in range(parts):
        recv1[part, seat] = send1[part, seat]

    t_index = lax.broadcasted_iota(jnp.int32, (tokens, tokens), 0)
    s_index = lax.broadcasted_iota(jnp.int32, (tokens, tokens), 1)
    causal = s_index <= t_index

    def local_mix(h):
        cols = span(h)
        column = jnp.concatenate([col_ref[h]] * (tokens // size), axis=1)
        gaps = column - run_ref[pl.ds(h, 1)]
        decay = jnp.where(causal, jnp.exp(jnp.where(causal, gaps, 0.0)), 0.0) * scaling
        dec_ref[h] = decay
        weights = (dot(q_ref[:, cols], k_ref[:, cols], 1, 1) * decay).astype(BF16)
        w_ref[h] = weights
        mix_ref[:, cols] = dot(weights, v_ref[:, cols], 1, 0)

    def group_sums(source, sums, part, backward):
        def group(o, carry):
            state = jnp.zeros((rows, size), F32)
            for step in range(half_inner):
                at = half_inner - 1 - step if backward else step
                factor = facs_ref[o * inner_size + half * half_inner + at]
                state = factor * state + source[part, o * half_inner + at]
            sums[part, half, o] = state
            return carry
        lax.fori_loop(0, outer_size, group, 0)

    def scan(source, sums, target, part, backward):
        order = (1, 0) if backward else (0, 1)

        def group(turn, carry):
            o = outer_size - 1 - turn if backward else turn
            entry = []
            for side in order:
                entry.append(carry)
                factor = facs_ref[o * inner_size + side * half_inner]
                for step in range(1, half_inner):
                    factor = factor * facs_ref[o * inner_size + side * half_inner + step]
                carry = factor * carry + sums[part, side, o]
            state = jnp.where(half == order[0], entry[0], entry[1])
            for step in range(half_inner):
                at = half_inner - 1 - step if backward else step
                target[part, o * half_inner + at] = state
                factor = facs_ref[o * inner_size + half * half_inner + at]
                state = factor * state + source[part, o * half_inner + at]
            return carry
        lax.fori_loop(0, outer_size, group, jnp.zeros((rows, size), F32))

    def carried(source, sums, target, result, phase, backward):
        for part in range(parts):
            drain(others(source, part), recv_sems.at[phase, part])
            group_sums(source, sums, part, backward)
            across(sums, phase + 1, part)
        for part in range(parts):
            drain(sums.at[part, 1 - half], recv_sems.at[phase + 1, part])
            scan(source, sums, target, part, backward)
            exchange(target, result, phase + 2, part)
            result[part, seat] = target[part, seat]

    loads[3].wait()
    drain(facs_ref.at[pl.ds(0, n - 1)], fac_sems.at[1])
    each_head(local_mix)
    carried(recv1, agg1, out1, ret1, 0, False)
    loads[4].wait()
    for part in range(parts):
        drain(others(ret1, part), recv_sems.at[2, part])

    def mix(h):
        cols = span(h)
        entering = get_state(ret1, h).astype(BF16)
        ent_ref[h] = entering
        growth = jnp.exp(col_ref[h])
        query_dec = (q_ref[:, cols].astype(F32) * growth).astype(BF16)
        mixed = mix_ref[:, cols] + scaling * dot(query_dec, entering, 1, 0)
        inverse = lax.rsqrt(jnp.mean(mixed * mixed, axis=1, keepdims=True) + EPSILON)
        normed = mixed * inverse
        att_ref[:, cols] = normed.astype(BF16)
        g = g_ref[:, cols].astype(F32)
        grad_mixed = (inverse * (g - normed * jnp.mean(g * normed, axis=1, keepdims=True))).astype(BF16)
        gm_ref[:, cols] = grad_mixed
        put_state(send2, h, scaling * dot(query_dec, grad_mixed, 0, 0))

    each_head(mix)
    for part in range(parts):
        exchange(send2, recv2, 3, part)
    for part in range(parts):
        recv2[part, seat] = send2[part, seat]

    def local_grads(h):
        cols = span(h)
        grad_mixed = gm_ref[:, cols]
        grad_score = (dot(grad_mixed, v_ref[:, cols], 1, 1) * dec_ref[h]).astype(BF16)
        far = (scaling * jnp.exp(col_ref[h])) * dot(grad_mixed, ent_ref[h], 1, 1)
        gq_ref[:, cols] = (dot(grad_score, k_ref[:, cols], 1, 0) + far).astype(BF16)
        gkl_ref[:, cols] = dot(grad_score, q_ref[:, cols], 0, 0)
        gvl_ref[:, cols] = dot(w_ref[h], grad_mixed, 0, 0)

    each_head(local_grads)
    carried(recv2, agg2, out2, ret2, 3, True)
    for part in range(parts):
        drain(others(ret2, part), recv_sems.at[5, part])

    def far_grads(h):
        cols = span(h)
        leaving = get_state(ret2, h).astype(BF16)
        shrink = jnp.exp(tot_ref[h] - col_ref[h])
        gk_ref[:, cols] = (gkl_ref[:, cols] + shrink * dot(v_ref[:, cols], leaving, 1, 1)).astype(BF16)
        gv_ref[:, cols] = (gvl_ref[:, cols] + dot(kd_ref[:, cols], leaving, 1, 0)).astype(BF16)

    each_head(far_grads)
    drain(facs_ref.at[pl.ds(0, n - 1)], fac_sems.at[0])
    for part in range(parts):
        for phase, buffer in ((0, send1), (2, out1), (3, send2), (5, out2)):
            drain(others(buffer, part), send_sems.at[phase, part])
        drain(agg1.at[part, half], send_sems.at[1, part])
        drain(agg2.at[part, half], send_sems.at[4, part])


def store(*refs):
    sources, targets, sems = refs[:4], refs[4:8], refs[8]
    copies = [pltpu.make_async_copy(s, t, sems.at[at]) for at, (s, t) in enumerate(zip(sources, targets))]
    for copy in copies:
        copy.start()
    for copy in copies:
        copy.wait()


def body(outer_size, inner_size, query_rows, key_rows, value_rows, log_decay, grad_out):
    n = outer_size * inner_size
    heads, tokens = log_decay.shape
    wide = query_rows.shape[1]
    size = wide // heads
    count = n // 2
    chunk = heads * size // count
    parts = PARTS if chunk % (8 * PARTS) == 0 else 1
    rows = chunk // parts
    pieces = pltpu.VMEM((parts, count, rows, size), F32)
    sums = pltpu.VMEM((parts, 2, outer_size, rows, size), F32)
    vmem = pl.BlockSpec(memory_space=pltpu.VMEM)
    hbm = pl.BlockSpec(memory_space=pltpu.HBM)
    row_block = pltpu.VMEM((tokens, wide), BF16)
    outs = [jax.ShapeDtypeStruct((tokens, wide), BF16)] * 4
    results = pl.pallas_call(
        functools.partial(kernel, outer_size, inner_size, parts),
        out_shape=outs,
        in_specs=[hbm] * 5,
        out_specs=[vmem] * 4,
        scratch_shapes=[
            row_block, row_block, row_block, pltpu.VMEM((heads, tokens), F32), row_block,
            pltpu.VMEM((heads, tokens), F32),
            pltpu.VMEM((heads, tokens, size), F32),
            pltpu.VMEM((heads, 1, size), F32),
            pltpu.VMEM((heads, 1, size), F32),
            pltpu.VMEM((n, 1, size), F32),
            pltpu.VMEM((heads, tokens, tokens), F32),
            pltpu.VMEM((heads, tokens, tokens), BF16),
            row_block,
            pltpu.VMEM((tokens, wide), F32),
            row_block,
            pieces, pieces, pieces, pieces, sums, pieces, pieces, pieces, pieces, sums,
            pltpu.VMEM((heads, size, size), BF16),
            pltpu.VMEM((tokens, wide), F32),
            pltpu.VMEM((tokens, wide), F32),
            pltpu.SemaphoreType.DMA((5,)),
            pltpu.SemaphoreType.DMA((2,)),
            pltpu.SemaphoreType.DMA((6, parts)),
            pltpu.SemaphoreType.DMA((6, parts)),
        ],
        compiler_params=pltpu.CompilerParams(
            collective_id=0, has_side_effects=True, vmem_limit_bytes=40 * 1024 * 1024),
    )(*[pltpu.with_memory_space_constraint(x, pltpu.HBM) for x in (query_rows, key_rows, value_rows, log_decay, grad_out)])
    return pl.pallas_call(
        store,
        out_shape=outs,
        in_specs=[vmem] * 4,
        out_specs=[hbm] * 4,
        scratch_shapes=[pltpu.SemaphoreType.DMA((4,))],
        compiler_params=pltpu.CompilerParams(vmem_limit_bytes=8 * 1024 * 1024),
    )(*results)


def solution(mesh):
    both = ("outer", "inner")
    row_spec = P(both, None)
    return jax.shard_map(
        functools.partial(body, mesh.shape["outer"], mesh.shape["inner"]),
        mesh=mesh,
        in_specs=(row_spec, row_spec, row_spec, P(None, both), row_spec),
        out_specs=(row_spec,) * 4,
        check_vma=False,
    )
```

profile of v0, /device:TPU:0, one launch (start us, length us, event | category | flops | bytes accessed | tf_op | source)
XLA Modules:
  0.0 51.6 jit_solution(3038178433001219170)
XLA Ops:
  0.6 49.6 %shard_map.84 = (bf16[256,1024]{1,0:T(8,128)(2,1)S(1)}, bf16[256,1024]{1,0:T(8,128)(2,1)S(1)}, bf16[256,1024]{1,0:T(8,128)(2,1)S(1)}, bf16[256,1024]{1,0:T(8,128)(2,1)S(1)}) custom-call(bf16[256,1024]{1,0:T(8,128)(2,1)} %q_hbm.1, bf16[256,1024]{1,0:T(8,128)(2,1)} %k_hbm.1, bf16[256,1024]{1,0:T(8,128)(2,1)} %v_hbm.1, f32[8,256]{1,0:T(8,128)} %decay_hbm.1, ...), custom_call_target="tpu_custom_call" | custom-call | tf_op jit(solution)/shard_map/pallas_call | solution.py:284
  50.3 1.3 %shard_map.85 = (bf16[256,1024]{1,0:T(8,128)(2,1)}, bf16[256,1024]{1,0:T(8,128)(2,1)}, bf16[256,1024]{1,0:T(8,128)(2,1)}, bf16[256,1024]{1,0:T(8,128)(2,1)}) custom-call(bf16[256,1024]{1,0:T(8,128)(2,1)S(1)} %get-tuple-element.8.refs_0_, bf16[256,1024]{1,0:T(8,128)(2,1)S(1)} %get-tuple-element.9.refs_1_, bf16[256,1024]{1,0:T(8,128)(2,1)S(1)} %get-tuple-element.10.refs_2_, ...), custom_call_target="tpu_custom_call" | custom-call | tf_op jit(solution)/shard_map/pallas_call | solution.py:313
where the time goes:
time: 51.8 us; the launch traced here: 51.6 us
  Pallas kernels  51 us (98%)
  between operations  0.64 us (1%)
    pallas_call x1, Pallas kernels, body(): pl.pallas_call(functools.partial(kernel, outer_size, inner_size, parts),...  49.6 us
    pallas_call x1, Pallas kernels, body(): pl.pallas_call(store, out_shape=outs, in_specs=[vmem] * 4, out_specs=[hbm...  1.35 us

commit v1 on v0

v1 whole, which is shorter than its diff:
```python
import functools
import math

import jax
import jax.numpy as jnp
from jax import lax
from jax.experimental import pallas as pl
from jax.experimental.pallas import tpu as pltpu
from jax.sharding import PartitionSpec as P

EPSILON = 1e-06
F32 = jnp.float32
BF16 = jnp.bfloat16
MESH = pl.DeviceIdType.MESH
UNITS = 4
UNROLL = 16
PACE = 5.6
READY = {"S": 3.6, "C": 7.0, "M": 10.8, "G": 12.3, "BS": 16.4, "BC": 19.8, "F": 23.6}


def dot(a, b, da, db):
    return lax.dot_general(a, b, (((da,), (db,)), ((), ())), preferred_element_type=F32)


def kernel(outer_size, inner_size, units, q_hbm, k_hbm, v_hbm, decay_hbm, g_hbm,
           att_ref, gq_ref, gk_ref, gv_ref,
           q_ref, k_ref, v_ref, decay_ref, g_ref,
           run_ref, col_ref, tot_ref, fac_ref, facs_ref, spread_ref, dec_ref, w_ref, kd_ref, mix_ref, gm_ref,
           send1, recv1, out1, ret1, agg1, send2, recv2, out2, ret2, agg2, ent_ref, gkl_ref, gvl_ref,
           load_sems, fac_sems, send_sems, recv_sems):
    n = outer_size * inner_size
    half_inner = inner_size // 2
    count = n // 2
    heads, tokens = decay_ref.shape
    size = q_ref.shape[1] // heads
    scaling = 1.0 / math.sqrt(size)
    per_unit = heads // units
    rows = per_unit * size // count
    lanes = size // heads
    place_o, place_i = lax.axis_index("outer"), lax.axis_index("inner")
    half = lax.div(place_i, half_inner)
    near = lax.rem(place_i, half_inner)
    seat = place_o * half_inner + near
    mine = lax.div(seat * rows, size)
    partner = (place_o, lax.rem(place_i + half_inner, inner_size))

    def unit_heads(u):
        return range(u * per_unit, (u + 1) * per_unit)

    def unit_span(u):
        return pl.ds(u * per_unit * size, per_unit * size)

    def span(h):
        return pl.ds(h * size, size)

    decay_load = pltpu.make_async_copy(decay_hbm, decay_ref, load_sems.at[0, 0])
    decay_load.start()
    loads = {}
    for at, (name, source, target) in enumerate(
            (("k", k_hbm, k_ref), ("v", v_hbm, v_ref), ("q", q_hbm, q_ref), ("g", g_hbm, g_ref))):
        for u in range(units):
            loads[name, u] = pltpu.make_async_copy(
                source.at[:, unit_span(u)], target.at[:, unit_span(u)], load_sems.at[at + 1, u])
    for u in range(units):
        loads["k", u].start()
        loads["v", u].start()

    shifts = [(do, di) for do in range(outer_size) for di in range(half_inner) if do or di]
    shifts.sort(key=lambda s: (s[1] % 2 == 0, s[0] % 2 == 0, s[0] == 0))
    far = [s for s in shifts if s[1] % 2]
    close = [s for s in shifts if not s[1] % 2]
    shifts = [s for pair in zip(far, close) for s in pair] + far[len(close):] + close[len(far):]

    def peers(act):
        def one(do, di):
            o = lax.rem(place_o + do, outer_size)
            i = lax.rem(near + di, half_inner)
            act(o, half * half_inner + i, o * half_inner + i)

        if count <= UNROLL:
            for do, di in shifts:
                one(do, di)
        else:
            def turn(step, carry):
                one(lax.rem(step + 1, outer_size), lax.div(step + 1, outer_size))
                return carry
            lax.fori_loop(0, count - 1, turn, 0)

    barrier = pltpu.get_barrier_semaphore()
    peers(lambda o, i, s: pl.semaphore_signal(barrier, inc=1, device_id=(o, i), device_id_type=MESH))
    pl.semaphore_signal(barrier, inc=1, device_id=partner, device_id_type=MESH)

    for name in ("q", "g"):
        for u in range(units):
            loads[name, u].start()

    def piece(buffer, u, s):
        return buffer.at[u, pl.ds(pl.multiple_of(s * rows, rows), rows)]

    def others(buffer, u):
        return buffer.at[u, pl.ds(0, (count - 1) * rows)]

    def exchange(source, target, phase, u):
        peers(lambda o, i, s: pltpu.make_async_remote_copy(
            src_ref=piece(source, u, s), dst_ref=piece(target, u, seat),
            send_sem=send_sems.at[phase, u], recv_sem=recv_sems.at[phase, u],
            device_id=(o, i), device_id_type=MESH).start())
        keep = pl.ds(pl.multiple_of(seat * rows, rows), rows)
        target[u, keep] = source[u, keep]

    def across(sums, phase, u):
        pltpu.make_async_remote_copy(
            src_ref=sums.at[u, half], dst_ref=sums.at[u, half],
            send_sem=send_sems.at[phase, u], recv_sem=recv_sems.at[phase, u],
            device_id=partner, device_id_type=MESH).start()

    def drain(piece, sem):
        pltpu.make_async_copy(piece, piece, sem).wait()

    decay_load.wait()
    running = decay_ref[...]
    lane = lax.broadcasted_iota(jnp.int32, (heads, tokens), 1)
    shift = 1
    while shift < tokens:
        running = running + jnp.where(lane >= shift, pltpu.roll(running, shift, 1), 0.0)
        shift *= 2
    run_ref[...] = running
    totals = jnp.broadcast_to(running[:, tokens - 1:], (heads, size))
    own = lax.broadcasted_iota(jnp.int32, (heads, size), 1) // lanes == lax.broadcasted_iota(jnp.int32, (heads, size), 0)
    fac_ref[...] = jnp.exp(jnp.sum(jnp.where(own, totals, 0.0), axis=0, keepdims=True))
    facs_ref[half, seat] = fac_ref[...]

    def state_of(u):
        loads["k", u].wait()
        loads["v", u].wait()
        for h in unit_heads(u):
            row = running[h:h + 1]
            column = jnp.broadcast_to(row, (size, tokens)).T
            col_ref[h] = column
            total = jnp.broadcast_to(row[:, tokens - 1:], (1, size))
            tot_ref[h] = total
            cols = span(h)
            key_dec = (k_ref[:, cols].astype(F32) * jnp.exp(total - column)).astype(BF16)
            kd_ref[:, cols] = key_dec
            send1[u, pl.ds((h - u * per_unit) * size, size)] = dot(key_dec, v_ref[:, cols], 0, 0)

    t_index = lax.broadcasted_iota(jnp.int32, (tokens, tokens), 0)
    s_index = lax.broadcasted_iota(jnp.int32, (tokens, tokens), 1)
    causal = s_index <= t_index

    def local_mix(u):
        loads["q", u].wait()
        for h in unit_heads(u):
            cols = span(h)
            column = jnp.concatenate([col_ref[h]] * (tokens // size), axis=1)
            gaps = column - run_ref[pl.ds(h, 1)]
            decay = jnp.where(causal, jnp.exp(jnp.where(causal, gaps, 0.0)), 0.0) * scaling
            dec_ref[h] = decay
            weights = (dot(q_ref[:, cols], k_ref[:, cols], 1, 1) * decay).astype(BF16)
            w_ref[h] = weights
            mix_ref[:, cols] = dot(weights, v_ref[:, cols], 1, 0)

    lane_of = lax.broadcasted_iota(jnp.int32, (count, size), 1)

    def spread(side):
        block = facs_ref[side].reshape(count, size)
        for u in range(units):
            one = jnp.sum(jnp.where(lane_of == (u * per_unit + mine) * lanes, block, 0.0), axis=1, keepdims=True)
            spread_ref[u, side] = jnp.broadcast_to(one, (count, size))

    def factor_of(u, side, s):
        return spread_ref[u, side, pl.ds(s, 1)]

    def fold(source, sums, u, phase, backward):
        drain(others(source, u), recv_sems.at[phase, u])
        for o in range(outer_size):
            state = None
            for step in range(half_inner):
                s = o * half_inner + (half_inner - 1 - step if backward else step)
                term = source[u, pl.ds(s * rows, rows)]
                state = term if state is None else factor_of(u, half, s) * state + term
            sums[u, half, o] = state
        across(sums, phase + 1, u)

    def scan(source, sums, target, result, u, phase, backward):
        drain(sums.at[u, 1 - half], recv_sems.at[phase + 1, u])
        order = (1, 0) if backward else (0, 1)
        carry = jnp.zeros((rows, size), F32)
        for turn in range(outer_size):
            o = outer_size - 1 - turn if backward else turn
            entry = []
            for side in order:
                entry.append(carry)
                factor = factor_of(u, side, o * half_inner)
                for step in range(1, half_inner):
                    factor = factor * factor_of(u, side, o * half_inner + step)
                carry = factor * carry + sums[u, side, o]
            state = jnp.where(half == order[0], entry[0], entry[1])
            for step in range(half_inner):
                s = o * half_inner + (half_inner - 1 - step if backward else step)
                target[u, pl.ds(s * rows, rows)] = state
                if step < half_inner - 1:
                    state = factor_of(u, half, s) * state + source[u, pl.ds(s * rows, rows)]
        exchange(target, result, phase + 2, u)

    def mix(u):
        drain(others(ret1, u), recv_sems.at[2, u])
        loads["g", u].wait()
        for h in unit_heads(u):
            cols = span(h)
            part = pl.ds((h - u * per_unit) * size, size)
            entering = ret1[u, part].astype(BF16)
            ent_ref[h] = entering
            growth = jnp.exp(col_ref[h])
            query_dec = (q_ref[:, cols].astype(F32) * growth).astype(BF16)
            mixed = mix_ref[:, cols] + scaling * dot(query_dec, entering, 1, 0)
            inverse = lax.rsqrt(jnp.mean(mixed * mixed, axis=1, keepdims=True) + EPSILON)
            normed = mixed * inverse
            att_ref[:, cols] = normed.astype(BF16)
            g = g_ref[:, cols].astype(F32)
            grad_mixed = (inverse * (g - normed * jnp.mean(g * normed, axis=1, keepdims=True))).astype(BF16)
            gm_ref[:, cols] = grad_mixed
            send2[u, part] = scaling * dot(query_dec, grad_mixed, 0, 0)
        exchange(send2, recv2, 3, u)

    def local_grads(u):
        for h in unit_heads(u):
            cols = span(h)
            grad_mixed = gm_ref[:, cols]
            grad_score = (dot(grad_mixed, v_ref[:, cols], 1, 1) * dec_ref[h]).astype(BF16)
            away = (scaling * jnp.exp(col_ref[h])) * dot(grad_mixed, ent_ref[h], 1, 1)
            gq_ref[:, cols] = (dot(grad_score, k_ref[:, cols], 1, 0) + away).astype(BF16)
            gkl_ref[:, cols] = dot(grad_score, q_ref[:, cols], 0, 0)
            gvl_ref[:, cols] = dot(w_ref[h], grad_mixed, 0, 0)

    def far_grads(u):
        drain(others(ret2, u), recv_sems.at[5, u])
        for h in unit_heads(u):
            cols = span(h)
            leaving = ret2[u, pl.ds((h - u * per_unit) * size, size)].astype(BF16)
            shrink = jnp.exp(tot_ref[h] - col_ref[h])
            gk_ref[:, cols] = (gkl_ref[:, cols] + shrink * dot(v_ref[:, cols], leaving, 1, 1)).astype(BF16)
            gv_ref[:, cols] = (gvl_ref[:, cols] + dot(kd_ref[:, cols], leaving, 1, 0)).astype(BF16)

    for u in range(units):
        state_of(u)
        if u == 0:
            pl.semaphore_wait(barrier, count)
        exchange(send1, recv1, 0, u)
        if u == 0:
            peers(lambda o, i, s: pltpu.make_async_remote_copy(
                src_ref=fac_ref, dst_ref=facs_ref.at[half, seat],
                send_sem=fac_sems.at[0], recv_sem=fac_sems.at[1],
                device_id=(o, i), device_id_type=MESH).start())
    for u in range(units):
        local_mix(u)
        if u == 0:
            drain(facs_ref.at[0, pl.ds(0, count - 1)], fac_sems.at[1])
            pltpu.make_async_remote_copy(
                src_ref=facs_ref.at[half], dst_ref=facs_ref.at[half],
                send_sem=fac_sems.at[2], recv_sem=fac_sems.at[3],
                device_id=partner, device_id_type=MESH).start()
            spread(half)

    def first_scan(u):
        if u == 0:
            drain(facs_ref.at[1 - half], fac_sems.at[3])
            spread(1 - half)
        scan(recv1, agg1, out1, ret1, u, 0, False)

    acts = {
        "S": lambda u: fold(recv1, agg1, u, 0, False),
        "C": first_scan,
        "M": mix,
        "G": local_grads,
        "BS": lambda u: fold(recv2, agg2, u, 3, True),
        "BC": lambda u: scan(recv2, agg2, out2, ret2, u, 3, True),
        "F": far_grads,
    }
    plan = sorted((READY[name] + PACE * u / units, name, u) for name in acts for u in range(units))
    for _, name, u in plan:
        acts[name](u)

    drain(facs_ref.at[0, pl.ds(0, count - 1)], fac_sems.at[0])
    drain(facs_ref.at[half], fac_sems.at[2])
    for u in range(units):
        for phase, buffer in ((0, send1), (2, out1), (3, send2), (5, out2)):
            drain(others(buffer, u), send_sems.at[phase, u])
        drain(agg1.at[u, half], send_sems.at[1, u])
        drain(agg2.at[u, half], send_sems.at[4, u])


def store(*refs):
    sources, targets, sems = refs[:4], refs[4:8], refs[8]
    copies = [pltpu.make_async_copy(s, t, sems.at[at]) for at, (s, t) in enumerate(zip(sources, targets))]
    for copy in copies:
        copy.start()
    for copy in copies:
        copy.wait()


def body(outer_size, inner_size, query_rows, key_rows, value_rows, log_decay, grad_out):
    n = outer_size * inner_size
    heads, tokens = log_decay.shape
    wide = query_rows.shape[1]
    size = wide // heads
    count = n // 2
    units = UNITS
    while units > 1 and (heads % units or (heads // units) * size % (8 * count)):
        units //= 2
    rows = heads // units * size // count
    pieces = pltpu.VMEM((units, count * rows, size), F32)
    sums = pltpu.VMEM((units, 2, outer_size, rows, size), F32)
    vmem = pl.BlockSpec(memory_space=pltpu.VMEM)
    hbm = pl.BlockSpec(memory_space=pltpu.HBM)
    row_block = pltpu.VMEM((tokens, wide), BF16)
    outs = [jax.ShapeDtypeStruct((tokens, wide), BF16)] * 4
    results = pl.pallas_call(
        functools.partial(kernel, outer_size, inner_size, units),
        out_shape=outs,
        in_specs=[hbm] * 5,
        out_specs=[vmem] * 4,
        scratch_shapes=[
            row_block, row_block, row_block, pltpu.VMEM((heads, tokens), F32), row_block,
            pltpu.VMEM((heads, tokens), F32),
            pltpu.VMEM((heads, tokens, size), F32),
            pltpu.VMEM((heads, 1, size), F32),
            pltpu.VMEM((1, size), F32),
            pltpu.VMEM((2, count, 1, size), F32),
            pltpu.VMEM((units, 2, count, size), F32),
            pltpu.VMEM((heads, tokens, tokens), F32),
            pltpu.VMEM((heads, tokens, tokens), BF16),
            row_block,
            pltpu.VMEM((tokens, wide), F32),
            row_block,
            pieces, pieces, pieces, pieces, sums, pieces, pieces, pieces, pieces, sums,
            pltpu.VMEM((heads, size, size), BF16),
            pltpu.VMEM((tokens, wide), F32),
            pltpu.VMEM((tokens, wide), F32),
            pltpu.SemaphoreType.DMA((5, units)),
            pltpu.SemaphoreType.DMA((4,)),
            pltpu.SemaphoreType.DMA((6, units)),
            pltpu.SemaphoreType.DMA((6, units)),
        ],
        compiler_params=pltpu.CompilerParams(
            collective_id=0, has_side_effects=True, vmem_limit_bytes=40 * 1024 * 1024),
    )(*[pltpu.with_memory_space_constraint(x, pltpu.HBM) for x in (query_rows, key_rows, value_rows, log_decay, grad_out)])
    return pl.pallas_call(
        store,
        out_shape=outs,
        in_specs=[vmem] * 4,
        out_specs=[hbm] * 4,
        scratch_shapes=[pltpu.SemaphoreType.DMA((4,))],
        compiler_params=pltpu.CompilerParams(vmem_limit_bytes=8 * 1024 * 1024),
    )(*results)


def solution(mesh):
    both = ("outer", "inner")
    row_spec = P(both, None)
    return jax.shard_map(
        functools.partial(body, mesh.shape["outer"], mesh.shape["inner"]),
        mesh=mesh,
        in_specs=(row_spec, row_spec, row_spec, P(None, both), row_spec),
        out_specs=(row_spec,) * 4,
        check_vma=False,
    )
```

time: 51.8 us -> 46.7 us (0.902)
  Pallas kernels: 51 us -> 45.9 us
    pallas_call x1, Pallas kernels: 49.6 us -> 44.5 us  [body(): pl.pallas_call(functools.partial(kernel, outer_size, inner_size, units),...]
where the time goes in v1:
time: 46.7 us; the launch traced here: 46.5 us
  Pallas kernels  45.9 us (98%)
  between operations  0.64 us (1%)
    pallas_call x1, Pallas kernels, body(): pl.pallas_call(functools.partial(kernel, outer_size, inner_size, units),...  44.5 us
    pallas_call x1, Pallas kernels, body(): pl.pallas_call(store, out_shape=outs, in_specs=[vmem] * 4, out_specs=[hbm...  1.35 us

profile of v1, /device:TPU:0, one launch (start us, length us, event | category | flops | bytes accessed | tf_op | source)
XLA Modules:
  0.0 46.5 jit_solution(10825309860698916101)
XLA Ops:
  0.6 44.5 %shard_map.84 = (bf16[256,1024]{1,0:T(8,128)(2,1)S(1)}, bf16[256,1024]{1,0:T(8,128)(2,1)S(1)}, bf16[256,1024]{1,0:T(8,128)(2,1)S(1)}, bf16[256,1024]{1,0:T(8,128)(2,1)S(1)}) custom-call(bf16[256,1024]{1,0:T(8,128)(2,1)} %q_hbm.1, bf16[256,1024]{1,0:T(8,128)(2,1)} %k_hbm.1, bf16[256,1024]{1,0:T(8,128)(2,1)} %v_hbm.1, f32[8,256]{1,0:T(8,128)} %decay_hbm.1, ...), custom_call_target="tpu_custom_call" | custom-call | tf_op jit(solution)/shard_map/pallas_call | solution.py:318
  45.2 1.3 %shard_map.85 = (bf16[256,1024]{1,0:T(8,128)(2,1)}, bf16[256,1024]{1,0:T(8,128)(2,1)}, bf16[256,1024]{1,0:T(8,128)(2,1)}, bf16[256,1024]{1,0:T(8,128)(2,1)}) custom-call(bf16[256,1024]{1,0:T(8,128)(2,1)S(1)} %get-tuple-element.8.refs_0_, bf16[256,1024]{1,0:T(8,128)(2,1)S(1)} %get-tuple-element.9.refs_1_, bf16[256,1024]{1,0:T(8,128)(2,1)S(1)} %get-tuple-element.10.refs_2_, ...), custom_call_target="tpu_custom_call" | custom-call | tf_op jit(solution)/shard_map/pallas_call | solution.py:348

commit v2 on v1

--- a/solution.py
+++ b/solution.py
@@ -12,17 +12,28 @@
 F32 = jnp.float32
 BF16 = jnp.bfloat16
 MESH = pl.DeviceIdType.MESH
-UNITS = 4
+SHARES = (2, 2, 2, 2)
 UNROLL = 16
-PACE = 5.6
-READY = {"S": 3.6, "C": 7.0, "M": 10.8, "G": 12.3, "BS": 16.4, "BC": 19.8, "F": 23.6}
+
+
+def plan(units):
+    every = range(units)
+    steps = [("A", 0), ("b", 0), ("f", 0), ("X", 0)]
+    for u in range(1, units):
+        steps += [("A", u), ("X", u)]
+    steps += [("L", u) for u in every] + [("r", 0)]
+    steps += [("S", u) for u in every] + [("C", u) for u in every]
+    for u in every:
+        steps += [("M", u), ("Y", u), ("G", u)]
+    steps += [(act, u) for act in "VWZ" for u in every]
+    return steps
 
 
 def dot(a, b, da, db):
     return lax.dot_general(a, b, (((da,), (db,)), ((), ())), preferred_element_type=F32)
 
 
-def kernel(outer_size, inner_size, units, q_hbm, k_hbm, v_hbm, decay_hbm, g_hbm,
+def kernel(outer_size, inner_size, shares, q_hbm, k_hbm, v_hbm, decay_hbm, g_hbm,
            att_ref, gq_ref, gk_ref, gv_ref,
            q_ref, k_ref, v_ref, decay_ref, g_ref,
            run_ref, col_ref, tot_ref, fac_ref, facs_ref, spread_ref, dec_ref, w_ref, kd_ref, mix_ref, gm_ref,
@@ -30,25 +41,26 @@
            load_sems, fac_sems, send_sems, recv_sems):
     n = outer_size * inner_size
     half_inner = inner_size // 2
+    extra = (outer_size + 7) // 8 * 8
     count = n // 2
     heads, tokens = decay_ref.shape
     size = q_ref.shape[1] // heads
     scaling = 1.0 / math.sqrt(size)
-    per_unit = heads // units
-    rows = per_unit * size // count
+    units = len(shares)
+    first = [sum(shares[:u]) for u in range(units)]
+    rows = [share * size // count for share in shares]
     lanes = size // heads
     place_o, place_i = lax.axis_index("outer"), lax.axis_index("inner")
     half = lax.div(place_i, half_inner)
     near = lax.rem(place_i, half_inner)
     seat = place_o * half_inner + near
-    mine = lax.div(seat * rows, size)
     partner = (place_o, lax.rem(place_i + half_inner, inner_size))
 
     def unit_heads(u):
-        return range(u * per_unit, (u + 1) * per_unit)
+        return range(first[u], first[u] + shares[u])
 
     def unit_span(u):
-        return pl.ds(u * per_unit * size, per_unit * size)
+        return pl.ds(first[u] * size, shares[u] * size)
 
     def span(h):
         return pl.ds(h * size, size)
@@ -66,7 +78,6 @@
         loads["v", u].start()
 
     shifts = [(do, di) for do in range(outer_size) for di in range(half_inner) if do or di]
-    shifts.sort(key=lambda s: (s[1] % 2 == 0, s[0] % 2 == 0, s[0] == 0))
     far = [s for s in shifts if s[1] % 2]
     close = [s for s in shifts if not s[1] % 2]
     shifts = [s for pair in zip(far, close) for s in pair] + far[len(close):] + close[len(far):]
@@ -94,23 +105,30 @@
         for u in range(units):
             loads[name, u].start()
 
-    def piece(buffer, u, s):
-        return buffer.at[u, pl.ds(pl.multiple_of(s * rows, rows), rows)]
+    def seat_rows(u, s):
+        return pl.ds(pl.multiple_of(first[u] * size + s * rows[u], 8), rows[u])
 
     def others(buffer, u):
-        return buffer.at[u, pl.ds(0, (count - 1) * rows)]
+        return buffer.at[pl.ds(first[u] * size, (count - 1) * rows[u])]
 
     def exchange(source, target, phase, u):
         peers(lambda o, i, s: pltpu.make_async_remote_copy(
-            src_ref=piece(source, u, s), dst_ref=piece(target, u, seat),
+            src_ref=source.at[seat_rows(u, s)], dst_ref=target.at[seat_rows(u, seat)],
             send_sem=send_sems.at[phase, u], recv_sem=recv_sems.at[phase, u],
             device_id=(o, i), device_id_type=MESH).start())
-        keep = pl.ds(pl.multiple_of(seat * rows, rows), rows)
-        target[u, keep] = source[u, keep]
+        target[seat_rows(u, seat)] = source[seat_rows(u, seat)]
+
+    starts = [outer_size * sum(rows[:u]) + extra * u for u in range(units)]
+    plain = [outer_size * sum(rows[:u]) for u in range(units)]
+
+    def side_sums(sums, side, u):
+        if sums is agg1:
+            return sums.at[side, pl.ds(starts[u], outer_size * rows[u] + extra)]
+        return sums.at[side, pl.ds(plain[u], outer_size * rows[u])]
 
     def across(sums, phase, u):
         pltpu.make_async_remote_copy(
-            src_ref=sums.at[u, half], dst_ref=sums.at[u, half],
+            src_ref=side_sums(sums, half, u), dst_ref=side_sums(sums, half, u),
             send_sem=send_sems.at[phase, u], recv_sem=recv_sems.at[phase, u],
             device_id=partner, device_id_type=MESH).start()
 
@@ -128,7 +146,7 @@
     totals = jnp.broadcast_to(running[:, tokens - 1:], (heads, size))
     own = lax.broadcasted_iota(jnp.int32, (heads, size), 1) // lanes == lax.broadcasted_iota(jnp.int32, (heads, size), 0)
     fac_ref[...] = jnp.exp(jnp.sum(jnp.where(own, totals, 0.0), axis=0, keepdims=True))
-    facs_ref[half, seat] = fac_ref[...]
+    facs_ref[seat] = fac_ref[...]
 
     def state_of(u):
         loads["k", u].wait()
@@ -142,7 +160,7 @@
             cols = span(h)
             key_dec = (k_ref[:, cols].astype(F32) * jnp.exp(total - column)).astype(BF16)
             kd_ref[:, cols] = key_dec
-            send1[u, pl.ds((h - u * per_unit) * size, size)] = dot(key_dec, v_ref[:, cols], 0, 0)
+            send1[pl.ds(h * size, size)] = dot(key_dec, v_ref[:, cols], 0, 0)
 
     t_index = lax.broadcasted_iota(jnp.int32, (tokens, tokens), 0)
     s_index = lax.broadcasted_iota(jnp.int32, (tokens, tokens), 1)
@@ -162,14 +180,20 @@
 
     lane_of = lax.broadcasted_iota(jnp.int32, (count, size), 1)
 
-    def spread(side):
-        block = facs_ref[side].reshape(count, size)
+    def spread():
+        block = facs_ref[...].reshape(count, size)
         for u in range(units):
-            one = jnp.sum(jnp.where(lane_of == (u * per_unit + mine) * lanes, block, 0.0), axis=1, keepdims=True)
-            spread_ref[u, side] = jnp.broadcast_to(one, (count, size))
-
-    def factor_of(u, side, s):
-        return spread_ref[u, side, pl.ds(s, 1)]
+            one = jnp.sum(jnp.where(lane_of == (first[u] + lax.div(seat * rows[u], size)) * lanes, block, 0.0), axis=1, keepdims=True)
+            spread_ref[u] = jnp.broadcast_to(one, (count, size))
+
+    def factor_of(u, s):
+        return spread_ref[u, pl.ds(s, 1)]
+
+    def group_rows(sums, u, o):
+        return pl.ds((starts if sums is agg1 else plain)[u] + o * rows[u], rows[u])
+
+    def product_row(u, o):
+        return pl.ds(starts[u] + outer_size * rows[u] + o, 1)
 
     def fold(source, sums, u, phase, backward):
         drain(others(source, u), recv_sems.at[phase, u])
@@ -177,30 +201,32 @@
             state = None
             for step in range(half_inner):
                 s = o * half_inner + (half_inner - 1 - step if backward else step)
-                term = source[u, pl.ds(s * rows, rows)]
-                state = term if state is None else factor_of(u, half, s) * state + term
-            sums[u, half, o] = state
+                term = source[seat_rows(u, s)]
+                state = term if state is None else factor_of(u, s) * state + term
+            sums[half, group_rows(sums, u, o)] = state
+            if not backward:
+                factor = factor_of(u, o * half_inner)
+                for step in range(1, half_inner):
+                    factor = factor * factor_of(u, o * half_inner + step)
+                sums[half, product_row(u, o)] = factor
         across(sums, phase + 1, u)
 
     def scan(source, sums, target, result, u, phase, backward):
-        drain(sums.at[u, 1 - half], recv_sems.at[phase + 1, u])
+        drain(side_sums(sums, 1 - half, u), recv_sems.at[phase + 1, u])
         order = (1, 0) if backward else (0, 1)
-        carry = jnp.zeros((rows, size), F32)
+        carry = jnp.zeros((rows[u], size), F32)
         for turn in range(outer_size):
             o = outer_size - 1 - turn if backward else turn
             entry = []
             for side in order:
                 entry.append(carry)
-                factor = factor_of(u, side, o * half_inner)
-                for step in range(1, half_inner):
-                    factor = factor * factor_of(u, side, o * half_inner + step)
-                carry = factor * carry + sums[u, side, o]
+                carry = agg1[side, product_row(u, o)] * carry + sums[side, group_rows(sums, u, o)]
             state = jnp.where(half == order[0], entry[0], entry[1])
             for step in range(half_inner):
                 s = o * half_inner + (half_inner - 1 - step if backward else step)
-                target[u, pl.ds(s * rows, rows)] = state
+                target[seat_rows(u, s)] = state
                 if step < half_inner - 1:
-                    state = factor_of(u, half, s) * state + source[u, pl.ds(s * rows, rows)]
+                    state = factor_of(u, s) * state + source[seat_rows(u, s)]
         exchange(target, result, phase + 2, u)
 
     def mix(u):
@@ -208,8 +234,8 @@
         loads["g", u].wait()
         for h in unit_heads(u):
             cols = span(h)
-            part = pl.ds((h - u * per_unit) * size, size)
-            entering = ret1[u, part].astype(BF16)
+            part = pl.ds(h * size, size)
+            entering = ret1[part].astype(BF16)
             ent_ref[h] = entering
             growth = jnp.exp(col_ref[h])
             query_dec = (q_ref[:, cols].astype(F32) * growth).astype(BF16)
@@ -220,8 +246,7 @@
             g = g_ref[:, cols].astype(F32)
             grad_mixed = (inverse * (g - normed * jnp.mean(g * normed, axis=1, keepdims=True))).astype(BF16)
             gm_ref[:, cols] = grad_mixed
-            send2[u, part] = scaling * dot(query_dec, grad_mixed, 0, 0)
-        exchange(send2, recv2, 3, u)
+            send2[part] = scaling * dot(query_dec, grad_mixed, 0, 0)
 
     def local_grads(u):
         for h in unit_heads(u):
@@ -237,57 +262,46 @@
         drain(others(ret2, u), recv_sems.at[5, u])
         for h in unit_heads(u):
             cols = span(h)
-            leaving = ret2[u, pl.ds((h - u * per_unit) * size, size)].astype(BF16)
+            leaving = ret2[pl.ds(h * size, size)].astype(BF16)
             shrink = jnp.exp(tot_ref[h] - col_ref[h])
             gk_ref[:, cols] = (gkl_ref[:, cols] + shrink * dot(v_ref[:, cols], leaving, 1, 1)).astype(BF16)
             gv_ref[:, cols] = (gvl_ref[:, cols] + dot(kd_ref[:, cols], leaving, 1, 0)).astype(BF16)
 
-    for u in range(units):
-        state_of(u)
-        if u == 0:
-            pl.semaphore_wait(barrier, count)
-        exchange(send1, recv1, 0, u)
-        if u == 0:
-            peers(lambda o, i, s: pltpu.make_async_remote_copy(
-                src_ref=fac_ref, dst_ref=facs_ref.at[half, seat],
-                send_sem=fac_sems.at[0], recv_sem=fac_sems.at[1],
-                device_id=(o, i), device_id_type=MESH).start())
-    for u in range(units):
-        local_mix(u)
-        if u == 0:
-            drain(facs_ref.at[0, pl.ds(0, count - 1)], fac_sems.at[1])
-            pltpu.make_async_remote_copy(
-                src_ref=facs_ref.at[half], dst_ref=facs_ref.at[half],
-                send_sem=fac_sems.at[2], recv_sem=fac_sems.at[3],
-                device_id=partner, device_id_type=MESH).start()
-            spread(half)
-
-    def first_scan(u):
-        if u == 0:
-            drain(facs_ref.at[1 - half], fac_sems.at[3])
-            spread(1 - half)
-        scan(recv1, agg1, out1, ret1, u, 0, False)
+    def send_factors():
+        peers(lambda o, i, s: pltpu.make_async_remote_copy(
+            src_ref=fac_ref, dst_ref=facs_ref.at[seat],
+            send_sem=fac_sems.at[0], recv_sem=fac_sems.at[1],
+            device_id=(o, i), device_id_type=MESH).start())
+
+    def take_factors():
+        drain(facs_ref.at[pl.ds(0, count - 1)], fac_sems.at[1])
+        spread()
 
     acts = {
+        "b": lambda u: pl.semaphore_wait(barrier, count),
+        "f": lambda u: send_factors(),
+        "r": lambda u: take_factors(),
+        "A": state_of,
+        "X": lambda u: exchange(send1, recv1, 0, u),
+        "L": local_mix,
         "S": lambda u: fold(recv1, agg1, u, 0, False),
-        "C": first_scan,
+        "C": lambda u: scan(recv1, agg1, out1, ret1, u, 0, False),
         "M": mix,
+        "Y": lambda u: exchange(send2, recv2, 3, u),
         "G": local_grads,
-        "BS": lambda u: fold(recv2, agg2, u, 3, True),
-        "BC": lambda u: scan(recv2, agg2, out2, ret2, u, 3, True),
-        "F": far_grads,
+        "V": lambda u: fold(recv2, agg2, u, 3, True),
+        "W": lambda u: scan(recv2, agg2, out2, ret2, u, 3, True),
+        "Z": far_grads,
     }
-    plan = sorted((READY[name] + PACE * u / units, name, u) for name in acts for u in range(units))
-    for _, name, u in plan:
-        acts[name](u)
-
-    drain(facs_ref.at[0, pl.ds(0, count - 1)], fac_sems.at[0])
-    drain(facs_ref.at[half], fac_sems.at[2])
+    for act, u in plan(units):
+        acts[act](u)
+
+    drain(facs_ref.at[pl.ds(0, count - 1)], fac_sems.at[0])
     for u in range(units):
         for phase, buffer in ((0, send1), (2, out1), (3, send2), (5, out2)):
             drain(others(buffer, u), send_sems.at[phase, u])
-        drain(agg1.at[u, half], send_sems.at[1, u])
-        drain(agg2.at[u, half], send_sems.at[4, u])
+        drain(side_sums(agg1, half, u), send_sems.at[1, u])
+        drain(side_sums(agg2, half, u), send_sems.at[4, u])
 
 
 def store(*refs):
@@ -305,18 +319,20 @@
     wide = query_rows.shape[1]
     size = wide // heads
     count = n // 2
-    units = UNITS
-    while units > 1 and (heads % units or (heads // units) * size % (8 * count)):
-        units //= 2
-    rows = heads // units * size // count
-    pieces = pltpu.VMEM((units, count * rows, size), F32)
-    sums = pltpu.VMEM((units, 2, outer_size, rows, size), F32)
+    shares = SHARES
+    if sum(shares) != heads or any(share * size % (8 * count) for share in shares):
+        shares = (heads,)
+    units = len(shares)
+    extra = (outer_size + 7) // 8 * 8
+    pieces = pltpu.VMEM((heads * size, size), F32)
+    sums = pltpu.VMEM((2, outer_size * heads * size // count, size), F32)
+    summed = pltpu.VMEM((2, outer_size * heads * size // count + extra * units, size), F32)
     vmem = pl.BlockSpec(memory_space=pltpu.VMEM)
     hbm = pl.BlockSpec(memory_space=pltpu.HBM)
     row_block = pltpu.VMEM((tokens, wide), BF16)
     outs = [jax.ShapeDtypeStruct((tokens, wide), BF16)] * 4
     results = pl.pallas_call(
-        functools.partial(kernel, outer_size, inner_size, units),
+        functools.partial(kernel, outer_size, inner_size, shares),
         out_shape=outs,
         in_specs=[hbm] * 5,
         out_specs=[vmem] * 4,
@@ -326,19 +342,19 @@
             pltpu.VMEM((heads, tokens, size), F32),
             pltpu.VMEM((heads, 1, size), F32),
             pltpu.VMEM((1, size), F32),
-            pltpu.VMEM((2, count, 1, size), F32),
-            pltpu.VMEM((units, 2, count, size), F32),
+            pltpu.VMEM((count, 1, size), F32),
+            pltpu.VMEM((units, count, size), F32),
             pltpu.VMEM((heads, tokens, tokens), F32),
             pltpu.VMEM((heads, tokens, tokens), BF16),
             row_block,
             pltpu.VMEM((tokens, wide), F32),
             row_block,
-            pieces, pieces, pieces, pieces, sums, pieces, pieces, pieces, pieces, sums,
+            pieces, pieces, pieces, pieces, summed, pieces, pieces, pieces, pieces, sums,
             pltpu.VMEM((heads, size, size), BF16),
             pltpu.VMEM((tokens, wide), F32),
             pltpu.VMEM((tokens, wide), F32),
             pltpu.SemaphoreType.DMA((5, units)),
-            pltpu.SemaphoreType.DMA((4,)),
+            pltpu.SemaphoreType.DMA((2,)),
             pltpu.SemaphoreType.DMA((6, units)),
             pltpu.SemaphoreType.DMA((6, units)),
         ],

time: 46.7 us -> 43 us (0.921)
  Pallas kernels: 45.9 us -> 42.1 us
    pallas_call x1, Pallas kernels: 44.5 us -> 40.8 us  [body(): pl.pallas_call(functools.partial(kernel, outer_size, inner_size, shares),...]
where the time goes in v2:
time: 43 us; the launch traced here: 42.7 us
  Pallas kernels  42.1 us (98%)
  between operations  0.64 us (1%)
    pallas_call x1, Pallas kernels, body(): pl.pallas_call(functools.partial(kernel, outer_size, inner_size, shares),...  40.8 us
    pallas_call x1, Pallas kernels, body(): pl.pallas_call(store, out_shape=outs, in_specs=[vmem] * 4, out_specs=[hbm...  1.35 us

profile of v2, /device:TPU:0, one launch (start us, length us, event | category | flops | bytes accessed | tf_op | source)
XLA Modules:
  0.0 42.7 jit_solution(2161884249367532195)
XLA Ops:
  0.6 40.8 %shard_map.84 = (bf16[256,1024]{1,0:T(8,128)(2,1)S(1)}, bf16[256,1024]{1,0:T(8,128)(2,1)S(1)}, bf16[256,1024]{1,0:T(8,128)(2,1)S(1)}, bf16[256,1024]{1,0:T(8,128)(2,1)S(1)}) custom-call(bf16[256,1024]{1,0:T(8,128)(2,1)} %q_hbm.1, bf16[256,1024]{1,0:T(8,128)(2,1)} %k_hbm.1, bf16[256,1024]{1,0:T(8,128)(2,1)} %v_hbm.1, f32[8,256]{1,0:T(8,128)} %decay_hbm.1, ...), custom_call_target="tpu_custom_call" | custom-call | tf_op jit(solution)/shard_map/pallas_call | solution.py:334
  41.4 1.3 %shard_map.85 = (bf16[256,1024]{1,0:T(8,128)(2,1)}, bf16[256,1024]{1,0:T(8,128)(2,1)}, bf16[256,1024]{1,0:T(8,128)(2,1)}, bf16[256,1024]{1,0:T(8,128)(2,1)}) custom-call(bf16[256,1024]{1,0:T(8,128)(2,1)S(1)} %get-tuple-element.8.refs_0_, bf16[256,1024]{1,0:T(8,128)(2,1)S(1)} %get-tuple-element.9.refs_1_, bf16[256,1024]{1,0:T(8,128)(2,1)S(1)} %get-tuple-element.10.refs_2_, ...), custom_call_target="tpu_custom_call" | custom-call | tf_op jit(solution)/shard_map/pallas_call | solution.py:364

commit v3 on v2

--- a/solution.py
+++ b/solution.py
@@ -14,6 +14,7 @@
 MESH = pl.DeviceIdType.MESH
 SHARES = (2, 2, 2, 2)
 UNROLL = 16
+ORDER = lambda m: (-(m[1] % 2), -(m[1] // 2), -(m[0] % 2), -(m[0] // 2))
 
 
 def plan(units):
@@ -22,7 +23,7 @@
     for u in range(1, units):
         steps += [("A", u), ("X", u)]
     steps += [("L", u) for u in every] + [("r", 0)]
-    steps += [("S", u) for u in every] + [("C", u) for u in every]
+    steps += [("S", u) for u in every] + [("t", 0)] + [("C", u) for u in every]
     for u in every:
         steps += [("M", u), ("Y", u), ("G", u)]
     steps += [(act, u) for act in "VWZ" for u in every]
@@ -36,12 +37,11 @@
 def kernel(outer_size, inner_size, shares, q_hbm, k_hbm, v_hbm, decay_hbm, g_hbm,
            att_ref, gq_ref, gk_ref, gv_ref,
            q_ref, k_ref, v_ref, decay_ref, g_ref,
-           run_ref, col_ref, tot_ref, fac_ref, facs_ref, spread_ref, dec_ref, w_ref, kd_ref, mix_ref, gm_ref,
+           run_ref, col_ref, shrink_ref, qd_ref, fac_ref, facs_ref, spread_ref, prod_ref, whole_ref, dec_ref, w_ref, kd_ref, mix_ref, gm_ref,
            send1, recv1, out1, ret1, agg1, send2, recv2, out2, ret2, agg2, ent_ref, gkl_ref, gvl_ref,
            load_sems, fac_sems, send_sems, recv_sems):
     n = outer_size * inner_size
     half_inner = inner_size // 2
-    extra = (outer_size + 7) // 8 * 8
     count = n // 2
     heads, tokens = decay_ref.shape
     size = q_ref.shape[1] // heads
@@ -77,23 +77,29 @@
         loads["k", u].start()
         loads["v", u].start()
 
-    shifts = [(do, di) for do in range(outer_size) for di in range(half_inner) if do or di]
-    far = [s for s in shifts if s[1] % 2]
-    close = [s for s in shifts if not s[1] % 2]
-    shifts = [s for pair in zip(far, close) for s in pair] + far[len(close):] + close[len(far):]
+    def flipped(place, mask):
+        bit = 1
+        while bit <= mask:
+            if mask & bit:
+                place = place + bit * (1 - 2 * lax.rem(lax.div(place, bit), 2))
+            bit *= 2
+        return place
+
+    binary = outer_size & (outer_size - 1) == 0 and half_inner & (half_inner - 1) == 0
+    masks = [(mo, mi) for mo in range(outer_size) for mi in range(half_inner) if mo or mi]
+    masks.sort(key=ORDER)
 
     def peers(act):
-        def one(do, di):
-            o = lax.rem(place_o + do, outer_size)
-            i = lax.rem(near + di, half_inner)
+        def one(o, i):
             act(o, half * half_inner + i, o * half_inner + i)
 
-        if count <= UNROLL:
-            for do, di in shifts:
-                one(do, di)
+        if binary and count <= UNROLL:
+            for mo, mi in masks:
+                one(flipped(place_o, mo), flipped(near, mi))
         else:
             def turn(step, carry):
-                one(lax.rem(step + 1, outer_size), lax.div(step + 1, outer_size))
+                one(lax.rem(place_o + lax.rem(step + 1, outer_size), outer_size),
+                    lax.rem(near + lax.div(step + 1, outer_size), half_inner))
                 return carry
             lax.fori_loop(0, count - 1, turn, 0)
 
@@ -118,12 +124,9 @@
             device_id=(o, i), device_id_type=MESH).start())
         target[seat_rows(u, seat)] = source[seat_rows(u, seat)]
 
-    starts = [outer_size * sum(rows[:u]) + extra * u for u in range(units)]
     plain = [outer_size * sum(rows[:u]) for u in range(units)]
 
     def side_sums(sums, side, u):
-        if sums is agg1:
-            return sums.at[side, pl.ds(starts[u], outer_size * rows[u] + extra)]
         return sums.at[side, pl.ds(plain[u], outer_size * rows[u])]
 
     def across(sums, phase, u):
@@ -156,9 +159,10 @@
             column = jnp.broadcast_to(row, (size, tokens)).T
             col_ref[h] = column
             total = jnp.broadcast_to(row[:, tokens - 1:], (1, size))
-            tot_ref[h] = total
             cols = span(h)
-            key_dec = (k_ref[:, cols].astype(F32) * jnp.exp(total - column)).astype(BF16)
+            shrink = jnp.exp(total - column)
+            shrink_ref[h] = shrink
+            key_dec = (k_ref[:, cols].astype(F32) * shrink).astype(BF16)
             kd_ref[:, cols] = key_dec
             send1[pl.ds(h * size, size)] = dot(key_dec, v_ref[:, cols], 0, 0)
 
@@ -177,6 +181,7 @@
             weights = (dot(q_ref[:, cols], k_ref[:, cols], 1, 1) * decay).astype(BF16)
             w_ref[h] = weights
             mix_ref[:, cols] = dot(weights, v_ref[:, cols], 1, 0)
+            qd_ref[:, cols] = (q_ref[:, cols].astype(F32) * jnp.exp(col_ref[h])).astype(BF16)
 
     lane_of = lax.broadcasted_iota(jnp.int32, (count, size), 1)
 
@@ -186,14 +191,19 @@
             one = jnp.sum(jnp.where(lane_of == (first[u] + lax.div(seat * rows[u], size)) * lanes, block, 0.0), axis=1, keepdims=True)
             spread_ref[u] = jnp.broadcast_to(one, (count, size))
 
+    def spread_products(side):
+        block = prod_ref[side]
+        lane_at = lax.broadcasted_iota(jnp.int32, block.shape, 1)
+        for u in range(units):
+            head = first[u] + lax.div(seat * rows[u], size)
+            one = jnp.sum(jnp.where(lane_at == head * lanes, block, 0.0), axis=1, keepdims=True)
+            whole_ref[u, side] = jnp.broadcast_to(one, block.shape)
+
     def factor_of(u, s):
         return spread_ref[u, pl.ds(s, 1)]
 
     def group_rows(sums, u, o):
-        return pl.ds((starts if sums is agg1 else plain)[u] + o * rows[u], rows[u])
-
-    def product_row(u, o):
-        return pl.ds(starts[u] + outer_size * rows[u] + o, 1)
+        return pl.ds(plain[u] + o * rows[u], rows[u])
 
     def fold(source, sums, u, phase, backward):
         drain(others(source, u), recv_sems.at[phase, u])
@@ -204,11 +214,6 @@
                 term = source[seat_rows(u, s)]
                 state = term if state is None else factor_of(u, s) * state + term
             sums[half, group_rows(sums, u, o)] = state
-            if not backward:
-                factor = factor_of(u, o * half_inner)
-                for step in range(1, half_inner):
-                    factor = factor * factor_of(u, o * half_inner + step)
-                sums[half, product_row(u, o)] = factor
         across(sums, phase + 1, u)
 
     def scan(source, sums, target, result, u, phase, backward):
@@ -220,7 +225,7 @@
             entry = []
             for side in order:
                 entry.append(carry)
-                carry = agg1[side, product_row(u, o)] * carry + sums[side, group_rows(sums, u, o)]
+                carry = whole_ref[u, side, pl.ds(o, 1)] * carry + sums[side, group_rows(sums, u, o)]
             state = jnp.where(half == order[0], entry[0], entry[1])
             for step in range(half_inner):
                 s = o * half_inner + (half_inner - 1 - step if backward else step)
@@ -237,8 +242,7 @@
             part = pl.ds(h * size, size)
             entering = ret1[part].astype(BF16)
             ent_ref[h] = entering
-            growth = jnp.exp(col_ref[h])
-            query_dec = (q_ref[:, cols].astype(F32) * growth).astype(BF16)
+            query_dec = qd_ref[:, cols]
             mixed = mix_ref[:, cols] + scaling * dot(query_dec, entering, 1, 0)
             inverse = lax.rsqrt(jnp.mean(mixed * mixed, axis=1, keepdims=True) + EPSILON)
             normed = mixed * inverse
@@ -263,8 +267,7 @@
         for h in unit_heads(u):
             cols = span(h)
             leaving = ret2[pl.ds(h * size, size)].astype(BF16)
-            shrink = jnp.exp(tot_ref[h] - col_ref[h])
-            gk_ref[:, cols] = (gkl_ref[:, cols] + shrink * dot(v_ref[:, cols], leaving, 1, 1)).astype(BF16)
+            gk_ref[:, cols] = (gkl_ref[:, cols] + shrink_ref[h] * dot(v_ref[:, cols], leaving, 1, 1)).astype(BF16)
             gv_ref[:, cols] = (gvl_ref[:, cols] + dot(kd_ref[:, cols], leaving, 1, 0)).astype(BF16)
 
     def send_factors():
@@ -275,12 +278,28 @@
 
     def take_factors():
         drain(facs_ref.at[pl.ds(0, count - 1)], fac_sems.at[1])
+        prod_ref[half] = jnp.zeros(prod_ref.shape[1:], F32)
+        for o in range(outer_size):
+            product = facs_ref[o * half_inner]
+            for step in range(1, half_inner):
+                product = product * facs_ref[o * half_inner + step]
+            prod_ref[half, pl.ds(o, 1)] = product
+        pltpu.make_async_remote_copy(
+            src_ref=prod_ref.at[half], dst_ref=prod_ref.at[half],
+            send_sem=fac_sems.at[2], recv_sem=fac_sems.at[3],
+            device_id=partner, device_id_type=MESH).start()
         spread()
+        spread_products(half)
+
+    def take_products():
+        drain(prod_ref.at[1 - half], fac_sems.at[3])
+        spread_products(1 - half)
 
     acts = {
         "b": lambda u: pl.semaphore_wait(barrier, count),
         "f": lambda u: send_factors(),
         "r": lambda u: take_factors(),
+        "t": lambda u: take_products(),
         "A": state_of,
         "X": lambda u: exchange(send1, recv1, 0, u),
         "L": local_mix,
@@ -297,6 +316,7 @@
         acts[act](u)
 
     drain(facs_ref.at[pl.ds(0, count - 1)], fac_sems.at[0])
+    drain(prod_ref.at[half], fac_sems.at[2])
     for u in range(units):
         for phase, buffer in ((0, send1), (2, out1), (3, send2), (5, out2)):
             drain(others(buffer, u), send_sems.at[phase, u])
@@ -306,7 +326,10 @@
 
 def store(*refs):
     sources, targets, sems = refs[:4], refs[4:8], refs[8]
-    copies = [pltpu.make_async_copy(s, t, sems.at[at]) for at, (s, t) in enumerate(zip(sources, targets))]
+    tokens = sources[0].shape[0]
+    cut = tokens // 1
+    copies = [pltpu.make_async_copy(s.at[pl.ds(c * cut, cut)], t.at[pl.ds(c * cut, cut)], sems.at[at, c])
+              for c in range(1) for at, (s, t) in enumerate(zip(sources, targets))]
     for copy in copies:
         copy.start()
     for copy in copies:
@@ -326,7 +349,6 @@
     extra = (outer_size + 7) // 8 * 8
     pieces = pltpu.VMEM((heads * size, size), F32)
     sums = pltpu.VMEM((2, outer_size * heads * size // count, size), F32)
-    summed = pltpu.VMEM((2, outer_size * heads * size // count + extra * units, size), F32)
     vmem = pl.BlockSpec(memory_space=pltpu.VMEM)
     hbm = pl.BlockSpec(memory_space=pltpu.HBM)
     row_block = pltpu.VMEM((tokens, wide), BF16)
@@ -340,21 +362,24 @@
             row_block, row_block, row_block, pltpu.VMEM((heads, tokens), F32), row_block,
             pltpu.VMEM((heads, tokens), F32),
             pltpu.VMEM((heads, tokens, size), F32),
-            pltpu.VMEM((heads, 1, size), F32),
+            pltpu.VMEM((heads, tokens, size), F32),
+            row_block,
             pltpu.VMEM((1, size), F32),
             pltpu.VMEM((count, 1, size), F32),
             pltpu.VMEM((units, count, size), F32),
+            pltpu.VMEM((2, extra, size), F32),
+            pltpu.VMEM((units, 2, extra, size), F32),
             pltpu.VMEM((heads, tokens, tokens), F32),
             pltpu.VMEM((heads, tokens, tokens), BF16),
             row_block,
             pltpu.VMEM((tokens, wide), F32),
             row_block,
-            pieces, pieces, pieces, pieces, summed, pieces, pieces, pieces, pieces, sums,
+            pieces, pieces, pieces, pieces, sums, pieces, pieces, pieces, pieces, sums,
             pltpu.VMEM((heads, size, size), BF16),
             pltpu.VMEM((tokens, wide), F32),
             pltpu.VMEM((tokens, wide), F32),
             pltpu.SemaphoreType.DMA((5, units)),
-            pltpu.SemaphoreType.DMA((2,)),
+            pltpu.SemaphoreType.DMA((4,)),
             pltpu.SemaphoreType.DMA((6, units)),
             pltpu.SemaphoreType.DMA((6, units)),
         ],
@@ -366,7 +391,7 @@
         out_shape=outs,
         in_specs=[vmem] * 4,
         out_specs=[hbm] * 4,
-        scratch_shapes=[pltpu.SemaphoreType.DMA((4,))],
+        scratch_shapes=[pltpu.SemaphoreType.DMA((4, 1))],
         compiler_params=pltpu.CompilerParams(vmem_limit_bytes=8 * 1024 * 1024),
     )(*results)
 

time: 43 us -> 41.5 us (0.965)
  Pallas kernels: 42.1 us -> 40.7 us
    pallas_call x1, Pallas kernels: 40.8 us -> 39.3 us  [body(): pl.pallas_call(functools.partial(kernel, outer_size, inner_size, shares),...]
where the time goes in v3:
time: 41.5 us; the launch traced here: 41.3 us
  Pallas kernels  40.7 us (98%)
  between operations  0.64 us (2%)
    pallas_call x1, Pallas kernels, body(): pl.pallas_call(functools.partial(kernel, outer_size, inner_size, shares),...  39.3 us
    pallas_call x1, Pallas kernels, body(): pl.pallas_call(store, out_shape=outs, in_specs=[vmem] * 4, out_specs=[hbm...  1.35 us

profile of v3, /device:TPU:0, one launch (start us, length us, event | category | flops | bytes accessed | tf_op | source)
XLA Modules:
  0.0 41.3 jit_solution(16390168131930997299)
XLA Ops:
  0.6 39.3 %shard_map.84 = (bf16[256,1024]{1,0:T(8,128)(2,1)S(1)}, bf16[256,1024]{1,0:T(8,128)(2,1)S(1)}, bf16[256,1024]{1,0:T(8,128)(2,1)S(1)}, bf16[256,1024]{1,0:T(8,128)(2,1)S(1)}) custom-call(bf16[256,1024]{1,0:T(8,128)(2,1)} %q_hbm.1, bf16[256,1024]{1,0:T(8,128)(2,1)} %k_hbm.1, bf16[256,1024]{1,0:T(8,128)(2,1)} %v_hbm.1, f32[8,256]{1,0:T(8,128)} %decay_hbm.1, ...), custom_call_target="tpu_custom_call" | custom-call | tf_op jit(solution)/shard_map/pallas_call | solution.py:356
  39.9 1.3 %shard_map.85 = (bf16[256,1024]{1,0:T(8,128)(2,1)}, bf16[256,1024]{1,0:T(8,128)(2,1)}, bf16[256,1024]{1,0:T(8,128)(2,1)}, bf16[256,1024]{1,0:T(8,128)(2,1)}) custom-call(bf16[256,1024]{1,0:T(8,128)(2,1)S(1)} %get-tuple-element.8.refs_0_, bf16[256,1024]{1,0:T(8,128)(2,1)S(1)} %get-tuple-element.9.refs_1_, bf16[256,1024]{1,0:T(8,128)(2,1)S(1)} %get-tuple-element.10.refs_2_, ...), custom_call_target="tpu_custom_call" | custom-call | tf_op jit(solution)/shard_map/pallas_call | solution.py:389

commit v4 on v3

--- a/solution.py
+++ b/solution.py
@@ -26,7 +26,7 @@
     steps += [("S", u) for u in every] + [("t", 0)] + [("C", u) for u in every]
     for u in every:
         steps += [("M", u), ("Y", u), ("G", u)]
-    steps += [(act, u) for act in "VWZ" for u in every]
+    steps += [(act, u) for act in "VWeZ" for u in every]
     return steps
 
 
@@ -312,24 +312,26 @@
         "W": lambda u: scan(recv2, agg2, out2, ret2, u, 3, True),
         "Z": far_grads,
     }
-    for act, u in plan(units):
-        acts[act](u)
-
-    drain(facs_ref.at[pl.ds(0, count - 1)], fac_sems.at[0])
-    drain(prod_ref.at[half], fac_sems.at[2])
-    for u in range(units):
-        for phase, buffer in ((0, send1), (2, out1), (3, send2), (5, out2)):
+    def finish_most(u):
+        for phase, buffer in ((0, send1), (2, out1), (3, send2)):
             drain(others(buffer, u), send_sems.at[phase, u])
         drain(side_sums(agg1, half, u), send_sems.at[1, u])
         drain(side_sums(agg2, half, u), send_sems.at[4, u])
 
+    acts["e"] = finish_most
+    drain_factors = ((facs_ref.at[pl.ds(0, count - 1)], fac_sems.at[0]), (prod_ref.at[half], fac_sems.at[2]))
+    for act, u in plan(units):
+        if (act, u) == ("e", 0):
+            for piece, sem in drain_factors:
+                drain(piece, sem)
+        acts[act](u)
+    for u in range(units):
+        drain(others(out2, u), send_sems.at[5, u])
+
 
 def store(*refs):
     sources, targets, sems = refs[:4], refs[4:8], refs[8]
-    tokens = sources[0].shape[0]
-    cut = tokens // 1
-    copies = [pltpu.make_async_copy(s.at[pl.ds(c * cut, cut)], t.at[pl.ds(c * cut, cut)], sems.at[at, c])
-              for c in range(1) for at, (s, t) in enumerate(zip(sources, targets))]
+    copies = [pltpu.make_async_copy(s, t, sems.at[at]) for at, (s, t) in enumerate(zip(sources, targets))]
     for copy in copies:
         copy.start()
     for copy in copies:
@@ -391,7 +393,7 @@
         out_shape=outs,
         in_specs=[vmem] * 4,
         out_specs=[hbm] * 4,
-        scratch_shapes=[pltpu.SemaphoreType.DMA((4, 1))],
+        scratch_shapes=[pltpu.SemaphoreType.DMA((4,))],
         compiler_params=pltpu.CompilerParams(vmem_limit_bytes=8 * 1024 * 1024),
     )(*results)
 

time: 41.5 us -> 41.5 us (level)
  no operation moved by 1% of the time
where the time goes in v4:
time: 41.5 us; the launch traced here: 41.3 us
  Pallas kernels  40.6 us (98%)
  between operations  0.64 us (2%)
    pallas_call x1, Pallas kernels, body(): pl.pallas_call(functools.partial(kernel, outer_size, inner_size, shares),...  39.3 us
    pallas_call x1, Pallas kernels, body(): pl.pallas_call(store, out_shape=outs, in_specs=[vmem] * 4, out_specs=[hbm...  1.35 us

profile of v4, /device:TPU:0, one launch (start us, length us, event | category | flops | bytes accessed | tf_op | source)
XLA Modules:
  0.0 41.3 jit_solution(7289823011668751560)
XLA Ops:
  0.6 39.3 %shard_map.84 = (bf16[256,1024]{1,0:T(8,128)(2,1)S(1)}, bf16[256,1024]{1,0:T(8,128)(2,1)S(1)}, bf16[256,1024]{1,0:T(8,128)(2,1)S(1)}, bf16[256,1024]{1,0:T(8,128)(2,1)S(1)}) custom-call(bf16[256,1024]{1,0:T(8,128)(2,1)} %q_hbm.1, bf16[256,1024]{1,0:T(8,128)(2,1)} %k_hbm.1, bf16[256,1024]{1,0:T(8,128)(2,1)} %v_hbm.1, f32[8,256]{1,0:T(8,128)} %decay_hbm.1, ...), custom_call_target="tpu_custom_call" | custom-call | tf_op jit(solution)/shard_map/pallas_call | solution.py:358
  39.9 1.3 %shard_map.85 = (bf16[256,1024]{1,0:T(8,128)(2,1)}, bf16[256,1024]{1,0:T(8,128)(2,1)}, bf16[256,1024]{1,0:T(8,128)(2,1)}, bf16[256,1024]{1,0:T(8,128)(2,1)}) custom-call(bf16[256,1024]{1,0:T(8,128)(2,1)S(1)} %get-tuple-element.8.refs_0_, bf16[256,1024]{1,0:T(8,128)(2,1)S(1)} %get-tuple-element.9.refs_1_, bf16[256,1024]{1,0:T(8,128)(2,1)S(1)} %get-tuple-element.10.refs_2_, ...), custom_call_target="tpu_custom_call" | custom-call | tf_op jit(solution)/shard_map/pallas_call | solution.py:391

commit v5 on v4

--- a/solution.py
+++ b/solution.py
@@ -22,8 +22,8 @@
     steps = [("A", 0), ("b", 0), ("f", 0), ("X", 0)]
     for u in range(1, units):
         steps += [("A", u), ("X", u)]
-    steps += [("L", u) for u in every] + [("r", 0)]
-    steps += [("S", u) for u in every] + [("t", 0)] + [("C", u) for u in every]
+    steps += [("L", u) for u in every[:-1]] + [("r", 0), ("S", 0), ("L", units - 1)]
+    steps += [("S", u) for u in every[1:]] + [("t", 0)] + [("C", u) for u in every]
     for u in every:
         steps += [("M", u), ("Y", u), ("G", u)]
     steps += [(act, u) for act in "VWeZ" for u in every]

time: 41.5 us -> 41.5 us (level)
  no operation moved by 1% of the time
where the time goes in v5:
time: 41.5 us; the launch traced here: 41.3 us
  Pallas kernels  40.6 us (98%)
  between operations  0.64 us (2%)
    pallas_call x1, Pallas kernels, body(): pl.pallas_call(functools.partial(kernel, outer_size, inner_size, shares),...  39.3 us
    pallas_call x1, Pallas kernels, body(): pl.pallas_call(store, out_shape=outs, in_specs=[vmem] * 4, out_specs=[hbm...  1.35 us

profile of v5, /device:TPU:0, one launch (start us, length us, event | category | flops | bytes accessed | tf_op | source)
XLA Modules:
  0.0 41.3 jit_solution(13230541856154204715)
XLA Ops:
  0.6 39.3 %shard_map.84 = (bf16[256,1024]{1,0:T(8,128)(2,1)S(1)}, bf16[256,1024]{1,0:T(8,128)(2,1)S(1)}, bf16[256,1024]{1,0:T(8,128)(2,1)S(1)}, bf16[256,1024]{1,0:T(8,128)(2,1)S(1)}) custom-call(bf16[256,1024]{1,0:T(8,128)(2,1)} %q_hbm.1, bf16[256,1024]{1,0:T(8,128)(2,1)} %k_hbm.1, bf16[256,1024]{1,0:T(8,128)(2,1)} %v_hbm.1, f32[8,256]{1,0:T(8,128)} %decay_hbm.1, ...), custom_call_target="tpu_custom_call" | custom-call | tf_op jit(solution)/shard_map/pallas_call | solution.py:358
  39.9 1.3 %shard_map.85 = (bf16[256,1024]{1,0:T(8,128)(2,1)}, bf16[256,1024]{1,0:T(8,128)(2,1)}, bf16[256,1024]{1,0:T(8,128)(2,1)}, bf16[256,1024]{1,0:T(8,128)(2,1)}) custom-call(bf16[256,1024]{1,0:T(8,128)(2,1)S(1)} %get-tuple-element.8.refs_0_, bf16[256,1024]{1,0:T(8,128)(2,1)S(1)} %get-tuple-element.9.refs_1_, bf16[256,1024]{1,0:T(8,128)(2,1)S(1)} %get-tuple-element.10.refs_2_, ...), custom_call_target="tpu_custom_call" | custom-call | tf_op jit(solution)/shard_map/pallas_call | solution.py:391
